TPU v7x, 32 devices: a whole 2x2x4 slice. The times are simulated.
32 devices in a mesh: chan: 8 (over z, y), period: 4 (over x, core).
Axes of the slice: x: 2, y: 2, z: 4, core: 2. Of those that a mesh axis runs over, the one named last changes fastest.
Arguments:
- raw_strain: bfloat16 [4, 2048, 512], P('period', 'chan'), may hold values from -16 to 16
- bin_ids: int32 [3, 512, 64], P(None, 'chan'), may hold values from 0 to 31, as said below
- owner_map: int32 [16], replicated, may hold values from 0 to 7, as said below
Outputs:
- stacks: float32 [32, 32, 256], P('chan')
Inputs may be any that keep to these rules, and one draw needn't show every extreme that they name: `bin_ids`: for channel c of block b = c // 64 and partner block b - d, the value is l * 8 + o: the pair lies in midpoint bin 2 * (b - 1) + l with l from 0 to 3, and in offset bin o below 8. `owner_map`: nondecreasing in the bin; bin m belongs to device m // 2 or m // 2 + 1; no device owns more than 4 bins and some device owns exactly 4.
All inputs are finite; a program needn't handle non-finite values.
Results may differ from a plain program's by a relative error of at most 0.0025.
Values may be sent and summed in bfloat16 or wider, within the bound.
A program may use at most 64 MiB of HBM per device.

v0:
```python
import functools
import math

import jax
import jax.numpy as jnp
import numpy as np
from jax import lax
from jax.experimental import pallas as pl
from jax.experimental.pallas import tpu as pltpu
from jax.sharding import PartitionSpec as P

CH_DEV = 64
WIN = 256
NF = 128
MB_DEV = 2
NOFF = 8
NP = 32


def passed_along(shard, axis, by):
    count = lax.axis_size(axis)
    pairs = [(i, i + by) for i in range(count) if 0 <= i + by < count]
    return lax.ppermute(shard, axis, pairs)


def with_halo(shard, sides, width):
    for axis, dim in sides:
        count, length = (lax.axis_size(axis), shard.shape[dim])
        up = [(i, (i + 1) % count) for i in range(count - 1)]
        down = [(j, i) for i, j in up]
        last = lax.slice_in_dim(shard, length - width, length, axis=dim)
        initial = lax.slice_in_dim(shard, 0, width, axis=dim)
        before = lax.ppermute(last, axis, up)
        after = lax.ppermute(initial, axis, down)
        shard = jnp.concatenate([before, shard, after], axis=dim)
    return shard


def dft_table():
    sample_at = jnp.arange(WIN, dtype=jnp.int32)[:, None]
    freq_at = jnp.arange(1, NF + 1, dtype=jnp.int32)[None, :]
    phase_angle = 2.0 * math.pi / WIN * jnp.mod(sample_at * freq_at, WIN).astype(jnp.float32)
    return jnp.concatenate([jnp.cos(phase_angle), -jnp.sin(phase_angle)], axis=1).astype(
        jnp.bfloat16
    )


def lag_table():
    freq_at = jnp.arange(1, NF + 1, dtype=jnp.int32)[:, None]
    lag_at = jnp.arange(WIN, dtype=jnp.int32)[None, :]
    phase_angle = 2.0 * math.pi / WIN * jnp.mod(freq_at * lag_at, WIN).astype(jnp.float32)
    return jnp.concatenate([jnp.cos(phase_angle), -jnp.sin(phase_angle)], axis=0)


def slant_tables():
    slow_at = (jnp.arange(NP, dtype=jnp.float32) - NP // 2) / (4.0 * NP)
    offset_at = (jnp.arange(NOFF, dtype=jnp.float32) + 0.5) * (3.0 * CH_DEV / NOFF)
    freq_at = jnp.arange(1, NF + 1, dtype=jnp.float32) * (2.0 * math.pi / WIN)
    phase_angle = slow_at[:, None, None] * offset_at[None, :, None] * freq_at[None, None, :]
    return (jnp.cos(phase_angle), jnp.sin(phase_angle))


def whiten_rows(spectra):
    power_mean = jnp.mean(spectra * spectra, axis=-1, keepdims=True)
    return (spectra / jnp.sqrt(power_mean + 1e-06)).astype(jnp.bfloat16)


def slant_lags(binned):
    cos_table, sin_table = slant_tables()
    highest = lax.Precision.HIGHEST
    real_part = binned[..., :NF]
    imag_part = binned[..., NF:]
    slant_real = jnp.einsum("mof,qof->mqf", real_part, cos_table, precision=highest) + jnp.einsum(
        "mof,qof->mqf", imag_part, sin_table, precision=highest
    )
    slant_imag = jnp.einsum("mof,qof->mqf", imag_part, cos_table, precision=highest) - jnp.einsum(
        "mof,qof->mqf", real_part, sin_table, precision=highest
    )
    slant_spec = jnp.concatenate([slant_real, slant_imag], axis=-1)
    return jnp.einsum("mqk,kt->mqt", slant_spec, lag_table(), precision=highest)


def normalize(total_trace):
    return total_trace / jnp.sqrt(
        jnp.mean(total_trace * total_trace, axis=-1, keepdims=True) + 1e-06
    )


def bin_pairs(own_spec, other_spec, pair_ids):
    freq_count = own_spec.shape[2] // 2
    channels = own_spec.shape[1]
    bin_count = 2 * MB_DEV * NOFF
    freq_block = min(32, freq_count)
    onehot = (
        lax.broadcasted_iota(jnp.int32, (bin_count, channels * channels), 0)
        == pair_ids.reshape(1, channels * channels)
    ).astype(jnp.bfloat16)
    real_cols = []
    imag_cols = []
    for freq_start in range(0, freq_count, freq_block):
        own_real = own_spec[:, :, freq_start : freq_start + freq_block]
        own_imag = own_spec[:, :, freq_count + freq_start : freq_count + freq_start + freq_block]
        other_real = other_spec[:, :, freq_start : freq_start + freq_block]
        other_imag = other_spec[
            :, :, freq_count + freq_start : freq_count + freq_start + freq_block
        ]
        left_side = jnp.stack(
            [
                jnp.concatenate([own_real, own_imag], axis=0),
                jnp.concatenate([own_imag, -own_real], axis=0),
            ]
        )
        right_side = jnp.concatenate([other_real, other_imag], axis=0)
        cross_block = jnp.einsum(
            "cwif,wjf->cfij", left_side, right_side, preferred_element_type=jnp.float32
        ).astype(jnp.bfloat16)
        flat_pairs = cross_block.reshape(2 * freq_block, channels * channels)
        binned_part = jnp.einsum(
            "np,rp->nr", onehot, flat_pairs, preferred_element_type=jnp.float32
        )
        real_cols.append(binned_part[:, :freq_block])
        imag_cols.append(binned_part[:, freq_block:])
    return jnp.concatenate(real_cols + imag_cols, axis=1)


def shards(raw_strain, bin_ids, owner_map):
    local_series = lax.all_to_all(raw_strain[0], "chan", split_axis=1, concat_axis=0, tiled=True)
    channels = local_series.shape[1]
    windows = local_series.reshape(local_series.shape[0] // WIN, WIN, channels)
    spectra = jnp.einsum("wtc,tk->wck", windows, dft_table(), preferred_element_type=jnp.float32)
    whitened = whiten_rows(spectra)
    near_spec = passed_along(whitened, "chan", 1)
    far_spec = passed_along(whitened, "chan", 2)
    partial_value = bin_pairs(whitened, whitened, bin_ids[0])
    partial_value = partial_value + bin_pairs(whitened, near_spec, bin_ids[1])
    partial_value = partial_value + bin_pairs(whitened, far_spec, bin_ids[2])
    beside_all = with_halo(partial_value[None], (("chan", 0),), 1)
    local_bins = 2 * MB_DEV
    capacity = 2 * MB_DEV
    device = lax.axis_index("chan")
    owned_count = jnp.sum((owner_map == device).astype(jnp.int32))
    first_bin = jnp.sum((owner_map < device).astype(jnp.int32))
    slot_at = lax.broadcasted_iota(jnp.int32, (capacity, 3, local_bins), 0)
    source_at = lax.broadcasted_iota(jnp.int32, (capacity, 3, local_bins), 1)
    place_at = lax.broadcasted_iota(jnp.int32, (capacity, 3, local_bins), 2)
    local_at = first_bin + slot_at - MB_DEV * (device + source_at - 2)
    select_rows = (
        ((local_at == place_at) & (slot_at < owned_count))
        .astype(jnp.float32)
        .reshape(capacity, 3 * local_bins)
    )
    stacked = beside_all.reshape(3 * local_bins, NOFF * 2 * NF)
    binned = jnp.dot(
        select_rows, stacked, precision=lax.Precision.HIGHEST, preferred_element_type=jnp.float32
    ).reshape(capacity, NOFF, 2 * NF)
    binned = lax.psum(binned, "period")
    total_trace = slant_lags(binned)
    return normalize(total_trace)


def host_tables():
    step = 2.0 * np.pi / WIN
    freq = np.arange(1, NF + 1)
    phase = step * np.mod(np.arange(WIN)[:, None] * freq[None, :], WIN)
    dft = np.concatenate([np.cos(phase), -np.sin(phase)], axis=1).astype(np.float32)
    lag = np.ascontiguousarray(dft_transposed(phase))
    slow = (np.arange(NP) - NP // 2) / (4.0 * NP)
    offset = (np.arange(NOFF) + 0.5) * (3.0 * CH_DEV / NOFF)
    angle = offset[:, None, None] * slow[None, :, None] * (freq * step)[None, None, :]
    return (
        dft.astype(jnp.bfloat16),
        lag,
        np.cos(angle).astype(np.float32),
        np.sin(angle).astype(np.float32),
    )


def dft_transposed(phase):
    return np.concatenate([np.cos(phase).T, -np.sin(phase).T], axis=0).astype(np.float32)


def flipped(me, by, count):
    result = 0
    bit = 1
    while bit < count:
        mine, other = (me // bit) % 2, (by // bit) % 2
        result = result + bit * (mine + other - 2 * mine * other)
        bit *= 2
    return result


GROUP = 64


def window_kernel(
    count, periods, bins, raw_hbm, ids_hbm, owner_hbm, dft_hbm, lag_hbm, cos_hbm, sin_hbm, out_ref,
    raw_ref, ids_ref, owner_ref, dft_ref, lag_ref, cos_ref, sin_ref, load_sem,
    id_buf, id_rows, spec, weights, held, part, part_send, part_recv, total_buf,
    id_send, id_recv, rs_send, rs_recv, ag_send, ag_recv,
):
    me = lax.axis_index("chan")
    period = lax.axis_index("period")
    local = 2 * MB_DEV * NOFF
    step_rows = MB_DEV * NOFF
    half = CH_DEV // 2
    mesh_id = pl.DeviceIdType.MESH

    barrier = pltpu.get_barrier_semaphore()

    def greet(t, unused):
        pl.semaphore_signal(barrier, inc=1, device_id=(flipped(me, t, count), period), device_id_type=mesh_id)
        return unused

    for t in reversed(range(1, count)):
        greet(t, 0)
    for t in range(1, periods):
        pl.semaphore_signal(barrier, inc=1, device_id=(me, (period + t) % periods), device_id_type=mesh_id)

    loads = []
    for k, (source, target) in enumerate(
        (
            (ids_hbm, ids_ref),
            (raw_hbm, raw_ref),
            (dft_hbm, dft_ref),
            (owner_hbm, owner_ref),
            (cos_hbm, cos_ref),
            (sin_hbm, sin_ref),
            (lag_hbm, lag_ref),
        )
    ):
        loads.append(pltpu.make_async_copy(source, target, load_sem.at[k]))
        loads[-1].start()

    weights[0 : 2 * CH_DEV] = jnp.zeros((2 * CH_DEV, 2 * NF), jnp.bfloat16)
    part[...] = jnp.zeros_like(part)
    loads[0].wait()
    near = jnp.concatenate([ids_ref[0], ids_ref[1]], axis=1)
    far = jnp.concatenate([ids_ref[2, :half], ids_ref[2, half:]], axis=1)
    id_buf[me] = jnp.concatenate([near, far], axis=0).astype(jnp.float32).astype(jnp.bfloat16)

    loads[1].wait()
    loads[2].wait()
    channels = count * CH_DEV
    chunk = min(128, channels)
    for start in range(0, channels, chunk):
        spectra = lax.dot_general(
            raw_ref[:, start : start + chunk],
            dft_ref[...],
            (((0,), (0,)), ((), ())),
            preferred_element_type=jnp.float32,
        )
        whitened = whiten_rows(spectra)
        weights[2 * CH_DEV + start : 2 * CH_DEV + start + chunk] = whitened
        spec[start : start + chunk] = whitened.astype(jnp.float32)

    def id_copy(t, source):
        return pltpu.make_async_remote_copy(
            src_ref=id_buf.at[me],
            dst_ref=id_buf.at[source],
            send_sem=id_send.at[t],
            recv_sem=id_recv.at[source],
            device_id=(flipped(me, t, count), period),
            device_id_type=mesh_id,
        )

    def send_ids(t, unused):
        id_copy(t, me).start()
        return unused

    bin_at = lax.broadcasted_iota(jnp.int32, (local, 4 * CH_DEV), 0).astype(jnp.float32)
    lane_at = lax.broadcasted_iota(jnp.int32, (half, 2 * CH_DEV), 1)

    def bin_block(block):
        ids = id_buf[block].astype(jnp.float32)
        id_rows[:, : 2 * CH_DEV] = ids[:CH_DEV]
        id_rows[:half, 2 * CH_DEV :] = jnp.where(lane_at < CH_DEV, ids[CH_DEV:], -1.0)
        id_rows[half:, 2 * CH_DEV :] = jnp.where(lane_at >= CH_DEV, ids[CH_DEV:], -1.0)
        for d, back in enumerate((0, 1, 2, 2)):
            at = pl.multiple_of((block + 2 - back) * CH_DEV, CH_DEV)
            held[d * CH_DEV : (d + 1) * CH_DEV] = weights[pl.ds(at, CH_DEV)]

        def group(g, carry):
            real, imag = carry
            first = g * GROUP
            hot = []
            for u in range(GROUP):
                row = id_rows[pl.ds(first + u, 1), :]
                hot.append(jnp.where(row == bin_at, 1.0, 0.0).astype(jnp.bfloat16))
            summed = jnp.dot(
                jnp.concatenate(hot, axis=0), held[...], preferred_element_type=jnp.float32
            )
            for u in range(GROUP):
                own = spec[pl.ds(block * CH_DEV + first + u, 1), :]
                own_real, own_imag = own[:, :NF], own[:, NF:]
                other_real = summed[u * local : (u + 1) * local, :NF]
                other_imag = summed[u * local : (u + 1) * local, NF:]
                real = real + (own_real * other_real + own_imag * other_imag)
                imag = imag + (own_imag * other_real - own_real * other_imag)
            return real, imag

        zero = jnp.zeros((local, NF), jnp.float32)
        real, imag = (zero, zero)
        for g in range(CH_DEV // GROUP):
            real, imag = group(g, (real, imag))
        rows = pl.ds(pl.multiple_of(block * step_rows, step_rows), local)
        part[rows, :NF] += real
        part[rows, NF:] += imag

    def part_copy(to, source):
        return pltpu.make_async_remote_copy(
            src_ref=part_send.at[to],
            dst_ref=part_recv.at[source],
            send_sem=rs_send.at[to],
            recv_sem=rs_recv.at[source],
            device_id=(to, period),
            device_id_type=mesh_id,
        )

    bin_block(me)
    pl.semaphore_wait(barrier, count - 1 + periods - 1)
    lax.fori_loop(1, count, send_ids, 0)

    at_step = [flipped(me, block, count) for block in range(count)]
    done_at = []
    for to in range(count):
        last = at_step[to]
        if to > 0:
            last = jnp.maximum(last, at_step[to - 1])
        if to < count - 1:
            last = jnp.maximum(last, at_step[to + 1])
        done_at.append(jnp.where(me == to, -1, last))

    def one_block(t, unused):
        block = flipped(me, t, count)
        id_copy(t, block).wait_recv()
        bin_block(block)
        for to in range(count):

            @pl.when(done_at[to] == t)
            def _():
                part_send[to] = part[to * step_rows : to * step_rows + local].astype(part_send.dtype)
                part_copy(to, me).start()

        return unused

    lax.fori_loop(1, count, one_block, 0)

    def add_part(t, total):
        source = flipped(me, t, count)
        part_copy(me, source).wait_recv()
        return total + part_recv[source].astype(jnp.float32)

    mine = part[pl.ds(pl.multiple_of(me * step_rows, step_rows), local)]
    total_buf[period] = lax.fori_loop(1, count, add_part, mine).astype(total_buf.dtype)

    def total_copy(t, source):
        return pltpu.make_async_remote_copy(
            src_ref=total_buf.at[period],
            dst_ref=total_buf.at[source],
            send_sem=ag_send.at[t],
            recv_sem=ag_recv.at[source],
            device_id=(me, (period + t) % periods),
            device_id_type=mesh_id,
        )

    for t in range(1, periods):
        total_copy(t, period).start()

    for load in loads[3:]:
        load.wait()
    owned = jnp.int32(0)
    before = jnp.int32(0)
    for m in range(bins):
        owner = owner_ref[m]
        owned = owned + jnp.where(owner == me, 1, 0)
        before = before + jnp.where(owner < me, 1, 0)
    skipped = before - MB_DEV * (me - 1)

    for t in range(1, periods):
        total_copy(t, (period + periods - t) % periods).wait_recv()
    total = total_buf[0].astype(jnp.float32)
    for p in range(1, periods):
        total = total + total_buf[p].astype(jnp.float32)

    capacity = 2 * MB_DEV
    slanted = []
    for slot in range(capacity):
        picked = jnp.zeros((NOFF, 2 * NF), jnp.float32)
        for c in range(2 * MB_DEV):
            wanted = jnp.where(slot < owned, skipped + slot, -1)
            picked = jnp.where(wanted == c, total[c * NOFF : (c + 1) * NOFF], picked)
        slant_real = jnp.zeros((NP, NF), jnp.float32)
        slant_imag = jnp.zeros((NP, NF), jnp.float32)
        for o in range(NOFF):
            real, imag = picked[o : o + 1, :NF], picked[o : o + 1, NF:]
            slant_real = slant_real + (real * cos_ref[o] + imag * sin_ref[o])
            slant_imag = slant_imag + (imag * cos_ref[o] - real * sin_ref[o])
        slanted.append(jnp.concatenate([slant_real, slant_imag], axis=1))
    traces = jnp.dot(
        jnp.concatenate(slanted, axis=0),
        lag_ref[...],
        precision=lax.Precision.HIGHEST,
        preferred_element_type=jnp.float32,
    )
    out_ref[...] = normalize(traces)

    def drain(t, unused):
        id_copy(t, me).wait_send()
        part_copy(flipped(me, t, count), me).wait_send()
        return unused

    lax.fori_loop(1, count, drain, 0)
    for t in range(1, periods):
        total_copy(t, period).wait_send()


def window_shards(count, periods, raw_strain, bin_ids, owner_map):
    local = 2 * MB_DEV * NOFF
    dft, lag, cos_table, sin_table = host_tables()
    vmem = pl.BlockSpec(memory_space=pltpu.VMEM)
    stacked = pl.pallas_call(
        functools.partial(window_kernel, count, periods, owner_map.shape[0]),
        out_shape=jax.ShapeDtypeStruct((2 * MB_DEV * NP, WIN), jnp.float32),
        in_specs=[pl.BlockSpec(memory_space=pl.ANY)] * 7,
        out_specs=vmem,
        scratch_shapes=[
            pltpu.VMEM(raw_strain.shape[1:], raw_strain.dtype),
            pltpu.VMEM(bin_ids.shape, bin_ids.dtype),
            pltpu.SMEM(owner_map.shape, owner_map.dtype),
            pltpu.VMEM(dft.shape, dft.dtype),
            pltpu.VMEM(lag.shape, lag.dtype),
            pltpu.VMEM(cos_table.shape, cos_table.dtype),
            pltpu.VMEM(sin_table.shape, sin_table.dtype),
            pltpu.SemaphoreType.DMA((7,)),
            pltpu.VMEM((count, CH_DEV + CH_DEV // 2, 2 * CH_DEV), jnp.bfloat16),
            pltpu.VMEM((CH_DEV, 4 * CH_DEV), jnp.float32),
            pltpu.VMEM((count * CH_DEV, 2 * NF), jnp.float32),
            pltpu.VMEM(((count + 2) * CH_DEV, 2 * NF), jnp.bfloat16),
            pltpu.VMEM((4 * CH_DEV, 2 * NF), jnp.bfloat16),
            pltpu.VMEM((count * MB_DEV * NOFF + local // 2, 2 * NF), jnp.float32),
            pltpu.VMEM((count, local, 2 * NF), jnp.bfloat16),
            pltpu.VMEM((count, local, 2 * NF), jnp.bfloat16),
            pltpu.VMEM((periods, local, 2 * NF), jnp.bfloat16),
            pltpu.SemaphoreType.DMA((count,)),
            pltpu.SemaphoreType.DMA((count,)),
            pltpu.SemaphoreType.DMA((count,)),
            pltpu.SemaphoreType.DMA((count,)),
            pltpu.SemaphoreType.DMA((periods,)),
            pltpu.SemaphoreType.DMA((periods,)),
        ],
        compiler_params=pltpu.CompilerParams(collective_id=0, has_side_effects=True),
    )(raw_strain[0], bin_ids, owner_map, dft, lag, cos_table, sin_table)
    return stacked.reshape(2 * MB_DEV, NP, WIN)


def device_shards(mesh, raw_strain, bin_ids, owner_map):
    count, periods = mesh.shape["chan"], mesh.shape["period"]
    if raw_strain.shape[1] == WIN and count & (count - 1) == 0:
        return window_shards(count, periods, raw_strain, bin_ids, owner_map)
    return shards(raw_strain, bin_ids, owner_map)


def solution(mesh):
    placed = (P("period", "chan", None), P(None, "chan", None), P())
    return jax.shard_map(
        functools.partial(device_shards, mesh),
        mesh=mesh,
        in_specs=placed,
        out_specs=P("chan", None, None),
        check_vma=False,
    )
```

profile of v0, /device:TPU:0, one launch (start us, length us, event | category | flops | bytes accessed | tf_op | source)
XLA Modules:
  0.0 23.3 jit_solution(15836652166731012869)
XLA Ops:
  0.0 21.7 %shard_map.73 = f32[128,256]{1,0:T(8,128)} custom-call(bf16[256,512]{1,0:T(8,128)(2,1)} %bitcast.3, s32[3,64,64]{2,1,0:T(8,128)} %ids_hbm.1, s32[16]{0:T(128)} %owner_hbm.1, bf16[256,256]{1,0:T(8,128)(2,1)} %constant.8.clone.dft_hbm, f32[256,256]{1,0:T(8,128)} %constant.9.clone.lag_hbm, f32[8,32,128]{2,1,0:T(8,128)} %constant.10.clone.cos_hbm, ...), custom_call_target="tpu_custom_call" | custom-call | tf_op jit(solution)/shard_map/pallas_call | solution.py:421
  21.8 1.6 %copy.9 = f32[4,32,256]{2,1,0:T(8,128)} copy(f32[4,32,256]{2,1,0:T(8,128)} %bitcast.2) | data formatting | bytes 262144
where the time goes:
time: 23.5 us; the launch traced here: 23.3 us
  Pallas kernels  21.7 us (92%)
  local copies, waits for them, and re-layouts  1.57 us (7%)
    pallas_call x1, Pallas kernels, window_shards(): pl.pallas_call(functools.partial(window_kernel, count, periods, owner_map...  21.7 us
    unnamed x1, local copies, waits for them, and re-layouts  1.57 us

commit v1 on v0

--- a/solution.py
+++ b/solution.py
@@ -195,32 +195,47 @@
 def window_kernel(
     count, periods, bins, raw_hbm, ids_hbm, owner_hbm, dft_hbm, lag_hbm, cos_hbm, sin_hbm, out_ref,
     raw_ref, ids_ref, owner_ref, dft_ref, lag_ref, cos_ref, sin_ref, load_sem,
-    id_buf, id_rows, spec, weights, held, part, part_send, part_recv, total_buf,
-    id_send, id_recv, rs_send, rs_recv, ag_send, ag_recv,
+    id_buf, id_rows, spec, weights, part, part_send, part_recv, acc, total_buf,
+    id_send, id_recv, raw_send, raw_recv, rs_send, rs_recv, ag_send, ag_recv,
 ):
+    scope = jax.named_scope
     me = lax.axis_index("chan")
     period = lax.axis_index("period")
+    side = lax.rem(period, 2)
+    pair = period - side
+    partner = pair + 1 - side
+    blocks = count // 2
+    width = (blocks + 2) * CH_DEV
     local = 2 * MB_DEV * NOFF
     step_rows = MB_DEV * NOFF
     half = CH_DEV // 2
     mesh_id = pl.DeviceIdType.MESH
+    near = lax.div(me, blocks) == side
+    mine = lax.rem(me, blocks)
+
+    ids_load = pltpu.make_async_copy(ids_hbm, ids_ref, load_sem.at[0])
+    ids_load.start()
 
     barrier = pltpu.get_barrier_semaphore()
 
-    def greet(t, unused):
-        pl.semaphore_signal(barrier, inc=1, device_id=(flipped(me, t, count), period), device_id_type=mesh_id)
-        return unused
-
-    for t in reversed(range(1, count)):
-        greet(t, 0)
-    for t in range(1, periods):
-        pl.semaphore_signal(barrier, inc=1, device_id=(me, (period + t) % periods), device_id_type=mesh_id)
+    def greet(chan, to):
+        pl.semaphore_signal(barrier, inc=1, device_id=(chan, to), device_id_type=mesh_id)
+
+    for t in range(1, count):
+        for s in range(2):
+            greet(lax.rem(me + t, count), pair + s)
+    greet(me, partner)
+    for j in range(2, periods, 2):
+        for s in range(2):
+            greet(me, lax.rem(pair + j, periods) + s)
+
+    def first_lane(which):
+        return pl.multiple_of(which * ((blocks - 2) * CH_DEV), 2 * CH_DEV)
 
     loads = []
     for k, (source, target) in enumerate(
         (
-            (ids_hbm, ids_ref),
-            (raw_hbm, raw_ref),
+            (raw_hbm.at[:, pl.ds(first_lane(side), width)], raw_ref.at[0]),
             (dft_hbm, dft_ref),
             (owner_hbm, owner_ref),
             (cos_hbm, cos_ref),
@@ -228,44 +243,70 @@
             (lag_hbm, lag_ref),
         )
     ):
-        loads.append(pltpu.make_async_copy(source, target, load_sem.at[k]))
+        loads.append(pltpu.make_async_copy(source, target, load_sem.at[k + 1]))
         loads[-1].start()
 
-    weights[0 : 2 * CH_DEV] = jnp.zeros((2 * CH_DEV, 2 * NF), jnp.bfloat16)
+    weights[0 : 2 * CH_DEV] = jnp.zeros((2 * CH_DEV, 4 * NF), jnp.bfloat16)
     part[...] = jnp.zeros_like(part)
-    loads[0].wait()
-    near = jnp.concatenate([ids_ref[0], ids_ref[1]], axis=1)
-    far = jnp.concatenate([ids_ref[2, :half], ids_ref[2, half:]], axis=1)
-    id_buf[me] = jnp.concatenate([near, far], axis=0).astype(jnp.float32).astype(jnp.bfloat16)
-
-    loads[1].wait()
-    loads[2].wait()
-    channels = count * CH_DEV
-    chunk = min(128, channels)
-    for start in range(0, channels, chunk):
-        spectra = lax.dot_general(
-            raw_ref[:, start : start + chunk],
-            dft_ref[...],
-            (((0,), (0,)), ((), ())),
-            preferred_element_type=jnp.float32,
-        )
-        whitened = whiten_rows(spectra)
-        weights[2 * CH_DEV + start : 2 * CH_DEV + start + chunk] = whitened
-        spec[start : start + chunk] = whitened.astype(jnp.float32)
-
-    def id_copy(t, source):
+
+    def id_copy(t, block):
         return pltpu.make_async_remote_copy(
-            src_ref=id_buf.at[me],
-            dst_ref=id_buf.at[source],
+            src_ref=id_buf.at[block],
+            dst_ref=id_buf.at[block],
             send_sem=id_send.at[t],
-            recv_sem=id_recv.at[source],
+            recv_sem=id_recv.at[block],
             device_id=(flipped(me, t, count), period),
             device_id_type=mesh_id,
         )
 
-    def send_ids(t, unused):
-        id_copy(t, me).start()
-        return unused
+    raw_copy = pltpu.make_async_remote_copy(
+        src_ref=raw_hbm.at[:, pl.ds(first_lane(1 - side), width)],
+        dst_ref=raw_ref.at[1],
+        send_sem=raw_send,
+        recv_sem=raw_recv,
+        device_id=(me, partner),
+        device_id_type=mesh_id,
+    )
+
+    with scope("w_ids"):
+        ids_load.wait()
+
+    @pl.when(near)
+    def _():
+        close = jnp.concatenate([ids_ref[0], ids_ref[1]], axis=1)
+        far = jnp.concatenate([ids_ref[2, :half], ids_ref[2, half:]], axis=1)
+        id_buf[mine] = jnp.concatenate([close, far], axis=0).astype(jnp.float32).astype(jnp.bfloat16)
+
+    with scope("w_barrier"):
+        pl.semaphore_wait(barrier, 2 * (count - 1) + 1 + periods - 2)
+
+    @pl.when(near)
+    def _():
+        for t in reversed(range(1, count)):
+            id_copy(t, mine).start()
+
+    raw_copy.start()
+
+    def whiten_window(k):
+        chunk = 2 * CH_DEV
+        for start in range(0, width, chunk):
+            spectra = lax.dot_general(
+                raw_ref[k, :, start : start + chunk],
+                dft_ref[...],
+                (((0,), (0,)), ((), ())),
+                preferred_element_type=jnp.float32,
+            )
+            whitened = whiten_rows(spectra)
+            columns = slice(k * 2 * NF, (k + 1) * 2 * NF)
+            weights[2 * CH_DEV + start : 2 * CH_DEV + start + chunk, columns] = whitened
+            spec[start : start + chunk, columns] = whitened.astype(jnp.float32)
+
+    loads[0].wait()
+    loads[1].wait()
+    whiten_window(0)
+    with scope("w_raw"):
+        raw_copy.wait_recv()
+    whiten_window(1)
 
     bin_at = lax.broadcasted_iota(jnp.int32, (local, 4 * CH_DEV), 0).astype(jnp.float32)
     lane_at = lax.broadcasted_iota(jnp.int32, (half, 2 * CH_DEV), 1)
@@ -275,98 +316,155 @@
         id_rows[:, : 2 * CH_DEV] = ids[:CH_DEV]
         id_rows[:half, 2 * CH_DEV :] = jnp.where(lane_at < CH_DEV, ids[CH_DEV:], -1.0)
         id_rows[half:, 2 * CH_DEV :] = jnp.where(lane_at >= CH_DEV, ids[CH_DEV:], -1.0)
-        for d, back in enumerate((0, 1, 2, 2)):
-            at = pl.multiple_of((block + 2 - back) * CH_DEV, CH_DEV)
-            held[d * CH_DEV : (d + 1) * CH_DEV] = weights[pl.ds(at, CH_DEV)]
-
-        def group(g, carry):
-            real, imag = carry
-            first = g * GROUP
+        own_block = block + 2 * side
+        held = jnp.concatenate(
+            [
+                weights[pl.ds(pl.multiple_of((own_block + 2 - back) * CH_DEV, CH_DEV), CH_DEV)]
+                for back in (0, 1, 2, 2)
+            ],
+            axis=0,
+        )
+
+        real = jnp.zeros((local, NF), jnp.float32)
+        imag = jnp.zeros((local, NF), jnp.float32)
+        for first in range(0, CH_DEV, GROUP):
             hot = []
             for u in range(GROUP):
-                row = id_rows[pl.ds(first + u, 1), :]
+                row = id_rows[first + u : first + u + 1, :]
                 hot.append(jnp.where(row == bin_at, 1.0, 0.0).astype(jnp.bfloat16))
             summed = jnp.dot(
-                jnp.concatenate(hot, axis=0), held[...], preferred_element_type=jnp.float32
+                jnp.concatenate(hot, axis=0), held, preferred_element_type=jnp.float32
             )
             for u in range(GROUP):
-                own = spec[pl.ds(block * CH_DEV + first + u, 1), :]
-                own_real, own_imag = own[:, :NF], own[:, NF:]
-                other_real = summed[u * local : (u + 1) * local, :NF]
-                other_imag = summed[u * local : (u + 1) * local, NF:]
-                real = real + (own_real * other_real + own_imag * other_imag)
-                imag = imag + (own_imag * other_real - own_real * other_imag)
-            return real, imag
-
-        zero = jnp.zeros((local, NF), jnp.float32)
-        real, imag = (zero, zero)
-        for g in range(CH_DEV // GROUP):
-            real, imag = group(g, (real, imag))
+                own = spec[pl.ds(own_block * CH_DEV + first + u, 1), :]
+                other = summed[u * local : (u + 1) * local]
+                for k in range(2):
+                    own_real = own[:, 2 * k * NF : (2 * k + 1) * NF]
+                    own_imag = own[:, (2 * k + 1) * NF : (2 * k + 2) * NF]
+                    other_real = other[:, 2 * k * NF : (2 * k + 1) * NF]
+                    other_imag = other[:, (2 * k + 1) * NF : (2 * k + 2) * NF]
+                    real = real + (own_real * other_real + own_imag * other_imag)
+                    imag = imag + (own_imag * other_real - own_real * other_imag)
         rows = pl.ds(pl.multiple_of(block * step_rows, step_rows), local)
         part[rows, :NF] += real
         part[rows, NF:] += imag
 
-    def part_copy(to, source):
+    first_pair = side * blocks - 1
+
+    def part_copy(k, upper):
         return pltpu.make_async_remote_copy(
-            src_ref=part_send.at[to],
-            dst_ref=part_recv.at[source],
-            send_sem=rs_send.at[to],
-            recv_sem=rs_recv.at[source],
-            device_id=(to, period),
+            src_ref=part_send.at[k],
+            dst_ref=part_recv.at[side, me],
+            send_sem=rs_send.at[2 * k + upper],
+            recv_sem=rs_recv.at[side, me],
+            device_id=(first_pair + k + 1 - upper, pair + upper),
             device_id_type=mesh_id,
         )
 
-    bin_block(me)
-    pl.semaphore_wait(barrier, count - 1 + periods - 1)
-    lax.fori_loop(1, count, send_ids, 0)
-
-    at_step = [flipped(me, block, count) for block in range(count)]
-    done_at = []
-    for to in range(count):
-        last = at_step[to]
-        if to > 0:
-            last = jnp.maximum(last, at_step[to - 1])
-        if to < count - 1:
-            last = jnp.maximum(last, at_step[to + 1])
-        done_at.append(jnp.where(me == to, -1, last))
+    def goes(k, upper):
+        owner = first_pair + k + 1 - upper
+        elsewhere = jnp.logical_or(owner != me, side != upper)
+        return (first_pair + k >= 0) & (owner < count) & elsewhere
+
+    base = jnp.where(near, mine, lax.rem(me, 2) + (1 - side) * (blocks - 2))
+    at_step = [flipped(base, block, blocks) for block in range(blocks)]
+    done_at = [at_step[0]]
+    done_at += [jnp.maximum(at_step[k - 1], at_step[k]) for k in range(1, blocks)]
+    done_at += [at_step[blocks - 1]]
 
     def one_block(t, unused):
-        block = flipped(me, t, count)
-        id_copy(t, block).wait_recv()
-        bin_block(block)
-        for to in range(count):
-
-            @pl.when(done_at[to] == t)
+        block = flipped(base, t, blocks)
+
+        @pl.when(jnp.logical_or(jnp.logical_not(near), t > 0))
+        def _():
+            with scope("w_id"):
+                id_copy(1, block).wait_recv()
+
+        with scope("bin"):
+            bin_block(block)
+        for k in range(blocks + 1):
+
+            @pl.when(done_at[k] == t)
             def _():
-                part_send[to] = part[to * step_rows : to * step_rows + local].astype(part_send.dtype)
-                part_copy(to, me).start()
+                part_send[k] = part[k * step_rows : (k + 1) * step_rows].astype(part_send.dtype)
+                for upper in range(2):
+
+                    @pl.when(goes(k, upper))
+                    def _():
+                        part_copy(k, upper).start()
 
         return unused
 
-    lax.fori_loop(1, count, one_block, 0)
-
-    def add_part(t, total):
-        source = flipped(me, t, count)
-        part_copy(me, source).wait_recv()
-        return total + part_recv[source].astype(jnp.float32)
-
-    mine = part[pl.ds(pl.multiple_of(me * step_rows, step_rows), local)]
-    total_buf[period] = lax.fori_loop(1, count, add_part, mine).astype(total_buf.dtype)
-
-    def total_copy(t, source):
+    lax.fori_loop(0, blocks, one_block, 0)
+
+    def part_arrival(from_side, source):
         return pltpu.make_async_remote_copy(
-            src_ref=total_buf.at[period],
+            src_ref=part_send.at[0],
+            dst_ref=part_recv.at[from_side, source],
+            send_sem=rs_send.at[0],
+            recv_sem=rs_recv.at[from_side, source],
+            device_id=(me, partner),
+            device_id_type=mesh_id,
+        )
+
+    kept = me - 1 + side
+    from_side = [
+        (kept >= 0) & (kept < blocks),
+        kept >= blocks - 1,
+    ]
+    from_own = jnp.where(side == 0, from_side[0], from_side[1])
+    at = jnp.clip(kept - first_pair, 0, blocks)
+    own_rows = part[pl.ds(pl.multiple_of(at * step_rows, step_rows), step_rows)]
+    acc[...] = jnp.where(from_own, own_rows, 0.0)
+    for s in range(2):
+
+        @pl.when(from_side[s] & (side != s))
+        def _():
+            with scope("w_part"):
+                part_arrival(s, me).wait_recv()
+            acc[...] += part_recv[s, me].astype(jnp.float32)
+
+        @pl.when(from_side[s])
+        def _():
+            total = acc[...]
+            for t in range(1, count):
+                source = flipped(me, t, count)
+                with scope("w_part"):
+                    part_arrival(s, source).wait_recv()
+                total = total + part_recv[s, source].astype(jnp.float32)
+            acc[...] = total
+
+    total_buf[period] = acc[...].astype(total_buf.dtype)
+
+    def total_copy(j, source):
+        return pltpu.make_async_remote_copy(
+            src_ref=total_buf.at[source],
             dst_ref=total_buf.at[source],
-            send_sem=ag_send.at[t],
+            send_sem=ag_send.at[j],
             recv_sem=ag_recv.at[source],
-            device_id=(me, (period + t) % periods),
+            device_id=(me, lax.rem(period + j, periods)),
             device_id_type=mesh_id,
         )
 
-    for t in range(1, periods):
-        total_copy(t, period).start()
-
-    for load in loads[3:]:
+    for j in range(1, periods):
+        total_copy(j, period).start()
+
+    with scope("drain"):
+
+        @pl.when(near)
+        def _():
+            for t in range(1, count):
+                id_copy(t, mine).wait_send()
+
+        raw_copy.wait_send()
+        for k in range(blocks + 1):
+            for upper in range(2):
+
+                @pl.when(goes(k, upper))
+                def _():
+                    part_copy(k, upper).wait_send()
+
+    for load in loads[2:]:
         load.wait()
     owned = jnp.int32(0)
     before = jnp.int32(0)
@@ -376,11 +474,16 @@
         before = before + jnp.where(owner < me, 1, 0)
     skipped = before - MB_DEV * (me - 1)
 
-    for t in range(1, periods):
-        total_copy(t, (period + periods - t) % periods).wait_recv()
-    total = total_buf[0].astype(jnp.float32)
-    for p in range(1, periods):
-        total = total + total_buf[p].astype(jnp.float32)
+    with scope("w_total"):
+        for j in range(1, periods):
+            total_copy(j, lax.rem(period + periods - j, periods)).wait_recv()
+    halves = []
+    for s in range(2):
+        total = total_buf[s].astype(jnp.float32)
+        for p in range(s + 2, periods, 2):
+            total = total + total_buf[p].astype(jnp.float32)
+        halves.append(total)
+    total = jnp.concatenate(halves, axis=0)
 
     capacity = 2 * MB_DEV
     slanted = []
@@ -402,51 +505,50 @@
         precision=lax.Precision.HIGHEST,
         preferred_element_type=jnp.float32,
     )
-    out_ref[...] = normalize(traces)
-
-    def drain(t, unused):
-        id_copy(t, me).wait_send()
-        part_copy(flipped(me, t, count), me).wait_send()
-        return unused
-
-    lax.fori_loop(1, count, drain, 0)
-    for t in range(1, periods):
-        total_copy(t, period).wait_send()
+    with scope("norm"):
+        out_ref[...] = normalize(traces)
+    for j in range(1, periods):
+        total_copy(j, period).wait_send()
 
 
 def window_shards(count, periods, raw_strain, bin_ids, owner_map):
     local = 2 * MB_DEV * NOFF
+    step_rows = MB_DEV * NOFF
+    blocks = count // 2
+    width = (blocks + 2) * CH_DEV
     dft, lag, cos_table, sin_table = host_tables()
-    vmem = pl.BlockSpec(memory_space=pltpu.VMEM)
+    dma = pltpu.SemaphoreType.DMA
     stacked = pl.pallas_call(
         functools.partial(window_kernel, count, periods, owner_map.shape[0]),
-        out_shape=jax.ShapeDtypeStruct((2 * MB_DEV * NP, WIN), jnp.float32),
+        out_shape=pltpu.VMEM((2 * MB_DEV * NP, WIN), jnp.float32),
         in_specs=[pl.BlockSpec(memory_space=pl.ANY)] * 7,
-        out_specs=vmem,
+        out_specs=pl.BlockSpec(memory_space=pltpu.VMEM),
         scratch_shapes=[
-            pltpu.VMEM(raw_strain.shape[1:], raw_strain.dtype),
+            pltpu.VMEM((2, WIN, width), raw_strain.dtype),
             pltpu.VMEM(bin_ids.shape, bin_ids.dtype),
             pltpu.SMEM(owner_map.shape, owner_map.dtype),
             pltpu.VMEM(dft.shape, dft.dtype),
             pltpu.VMEM(lag.shape, lag.dtype),
             pltpu.VMEM(cos_table.shape, cos_table.dtype),
             pltpu.VMEM(sin_table.shape, sin_table.dtype),
-            pltpu.SemaphoreType.DMA((7,)),
-            pltpu.VMEM((count, CH_DEV + CH_DEV // 2, 2 * CH_DEV), jnp.bfloat16),
+            dma((7,)),
+            pltpu.VMEM((blocks, CH_DEV + CH_DEV // 2, 2 * CH_DEV), jnp.bfloat16),
             pltpu.VMEM((CH_DEV, 4 * CH_DEV), jnp.float32),
-            pltpu.VMEM((count * CH_DEV, 2 * NF), jnp.float32),
-            pltpu.VMEM(((count + 2) * CH_DEV, 2 * NF), jnp.bfloat16),
-            pltpu.VMEM((4 * CH_DEV, 2 * NF), jnp.bfloat16),
-            pltpu.VMEM((count * MB_DEV * NOFF + local // 2, 2 * NF), jnp.float32),
-            pltpu.VMEM((count, local, 2 * NF), jnp.bfloat16),
-            pltpu.VMEM((count, local, 2 * NF), jnp.bfloat16),
-            pltpu.VMEM((periods, local, 2 * NF), jnp.bfloat16),
-            pltpu.SemaphoreType.DMA((count,)),
-            pltpu.SemaphoreType.DMA((count,)),
-            pltpu.SemaphoreType.DMA((count,)),
-            pltpu.SemaphoreType.DMA((count,)),
-            pltpu.SemaphoreType.DMA((periods,)),
-            pltpu.SemaphoreType.DMA((periods,)),
+            pltpu.VMEM((width, 4 * NF), jnp.float32),
+            pltpu.VMEM((width + 2 * CH_DEV, 4 * NF), jnp.bfloat16),
+            pltpu.VMEM(((blocks + 1) * step_rows, 2 * NF), jnp.float32),
+            pltpu.VMEM((blocks + 1, step_rows, 2 * NF), jnp.bfloat16),
+            pltpu.VMEM((2, count, step_rows, 2 * NF), jnp.bfloat16),
+            pltpu.VMEM((step_rows, 2 * NF), jnp.float32),
+            pltpu.VMEM((periods, step_rows, 2 * NF), jnp.bfloat16),
+            dma((count,)),
+            dma((blocks,)),
+            dma,
+            dma,
+            dma((2 * (blocks + 1),)),
+            dma((2, count)),
+            dma((periods,)),
+            dma((periods,)),
         ],
         compiler_params=pltpu.CompilerParams(collective_id=0, has_side_effects=True),
     )(raw_strain[0], bin_ids, owner_map, dft, lag, cos_table, sin_table)
@@ -455,7 +557,8 @@
 
 def device_shards(mesh, raw_strain, bin_ids, owner_map):
     count, periods = mesh.shape["chan"], mesh.shape["period"]
-    if raw_strain.shape[1] == WIN and count & (count - 1) == 0:
+    whole_windows = raw_strain.shape[1] == WIN and count >= 4 and count & (count - 1) == 0
+    if whole_windows and periods % 2 == 0:
         return window_shards(count, periods, raw_strain, bin_ids, owner_map)
     return shards(raw_strain, bin_ids, owner_map)
 

time: 23.5 us -> 21.9 us (0.932)
  local copies, waits for them, and re-layouts: 1.57 us -> 0.66 us
  Pallas kernels: 21.7 us -> 21.1 us
    unnamed x1, local copies, waits for them, and re-layouts: 1.57 us -> 0.66 us
    pallas_call x1, Pallas kernels: 21.7 us -> 21.1 us  [window_shards(): pl.pallas_call(functools.partial(window_kernel, count, periods, owner_map...]
where the time goes in v1:
time: 21.9 us; the launch traced here: 21.7 us
  Pallas kernels  21.1 us (96%)
  local copies, waits for them, and re-layouts  0.66 us (3%)
    pallas_call x1, Pallas kernels, window_shards(): pl.pallas_call(functools.partial(window_kernel, count, periods, owner_map...  21.1 us
    unnamed x1, local copies, waits for them, and re-layouts  0.66 us

profile of v1, /device:TPU:0, one launch (start us, length us, event | category | flops | bytes accessed | tf_op | source)
XLA Modules:
  0.0 21.7 jit_solution(12496135609944079177)
XLA Ops:
  0.0 21.1 %shard_map.73 = f32[128,256]{1,0:T(8,128)S(1)} custom-call(bf16[256,512]{1,0:T(8,128)(2,1)} %bitcast.3, s32[3,64,64]{2,1,0:T(8,128)} %ids_hbm.1, s32[16]{0:T(128)} %owner_hbm.1, bf16[256,256]{1,0:T(8,128)(2,1)} %constant.8.clone.dft_hbm, f32[256,256]{1,0:T(8,128)} %constant.9.clone.lag_hbm, f32[8,32,128]{2,1,0:T(8,128)} %constant.10.clone.cos_hbm, ...), custom_call_target="tpu_custom_call" | custom-call | tf_op jit(solution)/shard_map/pallas_call | solution.py:521
  21.1 0.7 %copy.9 = f32[4,32,256]{2,1,0:T(8,128)} copy(f32[4,32,256]{2,1,0:T(8,128)S(1)} %bitcast.2) | data formatting | bytes 262144
